TPU v7x, 32 devices: a whole 2x2x4 slice. The times are simulated.
32 devices in a mesh: dp: 4 (over z), rows: 8 (over y, x, core).
Axes of the slice: x: 2, y: 2, z: 4, core: 2. Of those that a mesh axis runs over, the one named last changes fastest.
Arguments:
- latent: bfloat16 [8, 8, 64, 640], P('dp', 'rows'), may hold values from -16.25 to 16.25
- hidden: bfloat16 [8, 8, 64, 640], P('dp', 'rows'), may hold values from -16.25 to 16.25
- cotangent: bfloat16 [8, 8, 64, 640], P('dp', 'rows'), may hold values from -6 to 6
- filter_one: bfloat16 [9, 640, 640], P(None, 'dp', 'rows'), may hold values from -0.078125 to 0.078125
- filter_two: bfloat16 [9, 640, 640], P(None, 'dp', 'rows'), may hold values from -0.078125 to 0.078125
- gain_one: float32 [640], replicated, may hold values from 0.1 to 1.9
- shift_one: float32 [640], replicated, may hold values from -2.5 to 2.5
- gain_two: float32 [640], replicated, may hold values from 0.1 to 1.9
- shift_two: float32 [640], replicated, may hold values from -2.5 to 2.5
Outputs:
- latent_grad: bfloat16 [8, 8, 64, 640], P('dp', 'rows')
All inputs are finite; a program needn't handle non-finite values.
Results may differ from a plain program's by a relative error of at most 0.0027.
Values may be sent and summed in bfloat16 or wider, within the bound.
A program may use at most 128 MiB of HBM per device.

v0:
```python
import jax
import jax.numpy as jnp
from jax import lax
from jax.sharding import PartitionSpec as P

GROUPS = 16
GSIZE = 40


def extended(block, sides, width):
    for axis, dim in sides:
        count = lax.axis_size(axis)
        forward = [(i, i + 1) for i in range(count - 1)]
        backward = [(target, source) for source, target in forward]
        low = lax.ppermute(
            lax.slice_in_dim(block, block.shape[dim] - width, None, axis=dim), axis, forward
        )
        high = lax.ppermute(lax.slice_in_dim(block, 0, width, axis=dim), axis, backward)
        block = jnp.concatenate([low, block, high], axis=dim)
    return block


def group_sums(values):
    per_channel = jnp.sum(values, axis=(1, 2))
    return jnp.sum(per_channel.reshape(per_channel.shape[0], GROUPS, -1), axis=2)


def expand_groups(moment):
    return jnp.repeat(moment, GSIZE, axis=1)[:, None, None, :]


def finish_stats(sum_plain, sum_square, number):
    average = sum_plain / number
    variance = sum_square / number - average * average
    return (average, lax.rsqrt(variance + 1e-05))


def reduced_stats(field, number):
    values = field.astype(jnp.float32)
    sum_plain, sum_square = lax.psum((group_sums(values), group_sums(values * values)), "rows")
    return finish_stats(sum_plain, sum_square, number)


def norm_backward(field, stats, gain, shift, incoming, number):
    average, inverse = stats
    values = field.astype(jnp.float32)
    normed = (values - expand_groups(average)) * expand_groups(inverse)
    linear = normed * gain + shift
    logistic = jax.nn.sigmoid(linear)
    scaled = incoming * logistic * (1.0 + linear * (1.0 - logistic)) * gain
    sum_first, sum_second = lax.psum((group_sums(scaled), group_sums(scaled * normed)), "rows")
    first = sum_first / number
    second = sum_second / number
    return expand_groups(inverse) * (scaled - expand_groups(first) - normed * expand_groups(second))


def conv_backward(gradient, weights):
    images, rows_here, breadth, channels = gradient.shape
    padded = extended(gradient, (("rows", 1),), 1)
    padded = jnp.pad(padded, ((0, 0), (0, 0), (1, 1), (0, 0)))
    pixels = images * rows_here * breadth
    shifted = []
    for tap_index in range(9):
        down_step = tap_index // 3 - 1
        side_step = tap_index % 3 - 1
        window = padded[
            :, 1 - down_step : 1 - down_step + rows_here, 1 - side_step : 1 - side_step + breadth, :
        ]
        shifted.append(window.reshape(pixels, channels))
    stacked = jnp.stack(shifted, axis=1)
    gathered = lax.all_gather(weights, "dp", axis=1, tiled=True)
    section = lax.all_gather(gathered, "rows", axis=2, tiled=True)
    columns = section.shape[2]
    window = stacked.reshape(pixels, 9 * columns)
    flat = jnp.transpose(section, (0, 2, 1)).reshape(9 * columns, section.shape[1])
    result = jnp.dot(window, flat, preferred_element_type=jnp.float32)
    return result.reshape(images, rows_here, breadth, channels)


def body(
    latent, hidden, cotangent, filter_one, filter_two, gain_one, shift_one, gain_two, shift_two
):
    number = latent.shape[1] * lax.axis_size("rows") * latent.shape[2] * GSIZE
    stats_two = reduced_stats(hidden, number)
    back_two = conv_backward(cotangent, filter_two)
    hidden_grad = norm_backward(hidden, stats_two, gain_two, shift_two, back_two, number).astype(
        jnp.bfloat16
    )
    stats_one = reduced_stats(latent, number)
    back_one = conv_backward(hidden_grad, filter_one)
    latent_part = norm_backward(latent, stats_one, gain_one, shift_one, back_one, number)
    return (cotangent.astype(jnp.float32) + latent_part).astype(jnp.bfloat16)


def solution(mesh):
    in_specs = (
        P("dp", "rows", None, None),
        P("dp", "rows", None, None),
        P("dp", "rows", None, None),
        P(None, "dp", "rows"),
        P(None, "dp", "rows"),
        P(),
        P(),
        P(),
        P(),
    )
    out_specs = P("dp", "rows", None, None)
    return jax.shard_map(body, mesh=mesh, in_specs=in_specs, out_specs=out_specs, check_vma=False)
```

profile of v0, /device:TPU:28, one launch (start us, length us, event | category | flops | bytes accessed | tf_op | source)
XLA Modules:
  0.0 223.1 jit_solution(1200964164859489196)
XLA Ops:
  6.5 1.2 copy.112
  7.7 47.0 %all_gather.12 = bf16[9,640,80]{2,0,1:T(8,128)(2,1)S(1)} all-gather(bf16[9,160,80]{2,0,1:T(8,128)(2,1)S(1)} %copy.112), channel_id=1, replica_groups=mesh['dp'=4,'rows'=8] {'dp'}, dimensions={1}, use_global_device_ids=true | all-gather | bytes 1152000 | tf_op jit(solution)/shard_map/all_gather | solution.py:71
  54.7 3.0 %copy.113 = bf16[9,640,80]{1,2,0:T(8,128)(2,1)} copy(bf16[9,640,80]{2,0,1:T(8,128)(2,1)S(1)} %all_gather.12) | data formatting | bytes 1843200 | tf_op jit(solution)/shard_map/all_gather | solution.py:71
  57.8 0.2 copy.123
  58.0 45.9 %all_gather.14 = bf16[9,640,80]{2,0,1:T(8,128)(2,1)S(1)} all-gather(bf16[9,160,80]{2,0,1:T(8,128)(2,1)S(1)} %copy.123), channel_id=1, replica_groups=mesh['dp'=4,'rows'=8] {'dp'}, dimensions={1}, use_global_device_ids=true | all-gather | bytes 1152000 | tf_op jit(solution)/shard_map/all_gather | solution.py:71
  103.8 3.0 %copy.124 = bf16[9,640,80]{1,2,0:T(8,128)(2,1)} copy(bf16[9,640,80]{2,0,1:T(8,128)(2,1)S(1)} %all_gather.14) | data formatting | bytes 1843200 | tf_op jit(solution)/shard_map/all_gather | solution.py:71
  106.9 2.1 collective-permute-start
  108.9 4.5 %collective-permute-start.1 = (bf16[2,1,64,640]{3,2,1,0:T(8,128)(2,1)S(1)}, bf16[2,1,64,640]{3,2,1,0:T(8,128)(2,1)S(1)}, u32[]{:S(2)}, u32[]{:S(2)}) collective-permute-start(bf16[2,1,64,640]{3,2,1,0:T(8,128)(2,1)S(1)} %copy-done), channel_id=1, source_target_pairs={{1,0},{2,1},{3,2},{4,3},{5,4},{6,5},{7,6},{9,8},{10,9},{11,10},{12... | collective-permute-start | bytes 491528 | tf_op jit(solution)/shard_map/ppermute | solution.py:18
  113.7 0.1 reduce_sum.149
  113.8 0.1 reduce_sum.151
  113.9 12.3 %all-reduce.4 = (f32[2,16]{1,0:T(2,128)S(1)}, f32[2,16]{1,0:T(2,128)S(1)}) all-reduce(f32[2,16]{1,0:T(2,128)S(1)} %reduce_sum.151, f32[2,16]{1,0:T(2,128)S(1)} %reduce_sum.149), channel_id=1, replica_groups=mesh['dp'=4,'rows'=8] {'rows'}, use_global_device_ids=true, to_apply=%region_11.12 | all-reduce | flops 64 | bytes 512 | tf_op jit(solution)/shard_map/psum | solution.py:40
  126.3 0.3 copy.107
  126.6 0.1 mul.122
  126.8 0.1 sub.60
  127.0 0.1 reduce_sum.145
  127.1 0.1 reshape.85
  127.2 0.1 reduce_sum.147
  127.3 0.2 fusion.15
  127.5 0.2 fusion.55
  127.6 0.3 copy.103
  127.9 1.0 copy.105
  128.9 1.0 copy.106
  129.8 1.0 copy.108
  130.8 1.0 copy.109
  131.8 1.0 copy.111
  132.8 1.0 copy.104
  133.8 1.0 copy.110
  134.8 11.1 %stack.6 = bf16[128,9,640]{2,1,0:T(8,128)(2,1)S(1)} concatenate(bf16[128,1,640]{2,1,0:T(2,128)(2,1)S(1)} %copy.103, bf16[128,1,640]{2,1,0:T(2,128)(2,1)} %copy.104, bf16[128,1,640]{2,1,0:T(2,128)(2,1)} %copy.105, bf16[128,1,640]{2,1,0:T(2,128)(2,1)} %copy.106, bf16[128,1,640]{2,1,0:T(2,128)(2,1)S(1)} %copy.107, bf16[128,1,640]{2,1,0:T(2,128)(2,1)} %copy.108, ...), dimensions={1} | concatenate | bytes 2949120 | tf_op jit(solution)/shard_map/stack | solution.py:70
  145.9 1.8 reshape.88
  147.7 5.1 %fusion.53 = (f32[2,640]{1,0:T(2,128)S(1)}, f32[2,640]{1,0:T(2,128)S(1)}, f32[2,1,64,640]{3,2,0,1:T(8,128)S(1)}) fusion(f32[2,640]{1,0:T(2,128)S(1)} %mul.122, f32[2,640]{1,0:T(2,128)S(1)} %sub.60, bf16[2,1,64,640]{3,2,1,0:T(8,128)(2,1)S(1)} %copy-done.4, f32[640]{0:T(1024)S(1)} %copy-done.6, f32[640]{0:T(1024)S(1)} %copy-done.7, ...), kind=kOutput, calls=%fused_computation.73 | convolution fusion | flops 945108480 | bytes 9364480 | tf_op jit(solution)/shard_map/dot_general | solution.py:76
  152.9 0.1 reduce_sum.153
  152.9 0.1 reshape.91
  153.0 0.1 reduce_sum.155
  153.1 12.0 %all-reduce.3 = (f32[2,16]{1,0:T(2,128)S(1)}, f32[2,16]{1,0:T(2,128)S(1)}, f32[2,16]{1,0:T(2,128)S(1)}, f32[2,16]{1,0:T(2,128)S(1)}) all-reduce(f32[2,16]{1,0:T(2,128)S(1)} %reduce_sum.155, f32[2,16]{1,0:T(2,128)S(1)} %reduce_sum.153, f32[2,16]{1,0:T(2,128)S(1)} %reduce_sum.147, ...), channel_id=1, replica_groups=mesh['dp'=4,'rows'=8] {'rows'}, use_global_device_ids=true, to_apply=%region_17.18 | all-reduce | flops 128 | bytes 1024 | tf_op jit(solution)/shard_map/psum | solution.py:51
  165.2 0.1 mul.132
  165.3 0.1 sub.64
  165.4 0.1 fusion.50
  165.5 1.9 collective-permute-start.2
  167.5 4.7 %collective-permute-start.3 = (bf16[2,1,64,640]{3,2,0,1:T(8,128)(2,1)S(1)}, bf16[2,1,64,640]{3,2,0,1:T(8,128)(2,1)S(1)}, u32[]{:S(2)}, u32[]{:S(2)}) collective-permute-start(bf16[2,1,64,640]{3,2,0,1:T(8,128)(2,1)S(1)} %fusion.50), channel_id=1, source_target_pairs={{1,0},{2,1},{3,2},{4,3},{5,4},{6,5},{7,6},{9,8},{10,9},{11,10},{12... | collective-permute-start | bytes 491528 | tf_op jit(solution)/shard_map/ppermute | solution.py:18
  172.2 0.3 copy.118
  172.5 0.1 mul.118
  172.7 0.1 sub.68
  172.8 1.2 collective-permute-done.2
  174.0 0.9 collective-permute-done.3
  174.8 0.2 fusion.17
  175.0 0.2 fusion.54
  175.1 0.3 copy.114
  175.4 1.0 copy.116
  176.4 1.0 copy.117
  177.4 1.0 copy.119
  178.4 1.0 copy.120
  179.4 1.0 copy.122
  180.3 1.0 copy.115
  181.3 1.0 copy.121
  182.3 11.0 %stack.7 = bf16[128,9,640]{2,1,0:T(8,128)(2,1)S(1)} concatenate(bf16[128,1,640]{2,1,0:T(2,128)(2,1)S(1)} %copy.114, bf16[128,1,640]{2,1,0:T(2,128)(2,1)} %copy.115, bf16[128,1,640]{2,1,0:T(2,128)(2,1)} %copy.116, bf16[128,1,640]{2,1,0:T(2,128)(2,1)} %copy.117, bf16[128,1,640]{2,1,0:T(2,128)(2,1)S(1)} %copy.118, bf16[128,1,640]{2,1,0:T(2,128)(2,1)} %copy.119, ...), dimensions={1} | concatenate | bytes 2949120 | tf_op jit(solution)/shard_map/stack | solution.py:70
  193.4 1.8 reshape.92
  195.2 4.9 %fusion.52 = (f32[2,640]{1,0:T(2,128)S(1)}, f32[2,640]{1,0:T(2,128)S(1)}, f32[2,1,64,640]{3,2,0,1:T(8,128)S(1)}) fusion(f32[2,640]{1,0:T(2,128)S(1)} %mul.118, f32[2,640]{1,0:T(2,128)S(1)} %sub.68, bf16[2,1,64,640]{3,2,1,0:T(8,128)(2,1)S(1)} %copy-done.2, f32[640]{0:T(1024)S(1)} %copy-done.8, f32[640]{0:T(1024)S(1)} %copy-done.9, ...), kind=kOutput, calls=%fused_computation.72 | convolution fusion | flops 945108480 | bytes 9364480 | tf_op jit(solution)/shard_map/dot_general | solution.py:76
  200.3 0.1 reduce_sum.157
  200.3 0.1 reshape.95
  200.4 0.1 reduce_sum.159
  200.5 14.6 %all-reduce.2 = (f32[2,16]{1,0:T(2,128)S(1)}, f32[2,16]{1,0:T(2,128)S(1)}) all-reduce(f32[2,16]{1,0:T(2,128)S(1)} %reduce_sum.159, f32[2,16]{1,0:T(2,128)S(1)} %reduce_sum.157), channel_id=1, replica_groups=mesh['dp'=4,'rows'=8] {'rows'}, use_global_device_ids=true, to_apply=%region_23.24 | all-reduce | flops 64 | bytes 512 | tf_op jit(solution)/shard_map/psum | solution.py:51
  215.2 0.1 mul.144
  215.4 0.1 sub.72
  215.5 0.8 fusion.51
  (48 shorter events, 1.3 us)
Async XLA Ops:
  6.5 141.2 %all-gather.3.cloned.1.call-start = ((), (), s32[]{:S(2)}) async-start(), calls=%async_computation | async-start | bytes 8294400 | tf_op jit(solution)/shard_map/all_gather | solution.py:72
  54.7 3.1 %copy-start.5 = (bf16[9,160,80]{2,1,0:T(8,128)(2,1)S(1)}, bf16[9,160,80]{2,1,0:T(8,128)(2,1)}, u32[]{:S(2)}) copy-start(bf16[9,160,80]{2,1,0:T(8,128)(2,1)} %param.12) | copy-start | bytes 691204
  57.7 137.5 %all-gather.5.cloned.1.call-start = ((), (), s32[]{:S(2)}) async-start(), calls=%async_computation.1 | async-start | bytes 8294400 | tf_op jit(solution)/shard_map/all_gather | solution.py:72
  103.8 3.0 %copy-start = (bf16[2,1,64,640]{3,2,1,0:T(8,128)(2,1)S(1)}, bf16[2,1,64,640]{3,2,1,0:T(8,128)(2,1)}, u32[]{:S(2)}) copy-start(bf16[2,1,64,640]{3,2,1,0:T(8,128)(2,1)} %param.11) | copy-start | bytes 491524
  103.8 9.6 %copy-start.3 = (bf16[2,1,64,640]{3,2,1,0:T(8,128)(2,1)S(1)}, bf16[2,1,64,640]{3,2,1,0:T(8,128)(2,1)}, u32[]{:S(2)}) copy-start(bf16[2,1,64,640]{3,2,1,0:T(8,128)(2,1)} %param.10) | copy-start | bytes 491524
  106.8 20.0 %copy-start.1 = (bf16[2,1,64,640]{3,2,1,0:T(8,128)(2,1)S(1)}, bf16[2,1,64,640]{3,2,1,0:T(8,128)(2,1)}, u32[]{:S(2)}) copy-start(bf16[2,1,64,640]{3,2,1,0:T(8,128)(2,1)} %param.9) | copy-start | bytes 491524
  106.9 20.4 %collective-permute-start = (bf16[2,1,64,640]{3,2,1,0:T(8,128)(2,1)S(1)}, bf16[2,1,64,640]{3,2,1,0:T(8,128)(2,1)S(1)}, u32[]{:S(2)}, u32[]{:S(2)}) collective-permute-start(bf16[2,1,64,640]{3,2,1,0:T(8,128)(2,1)S(1)} %copy-done), channel_id=1, source_target_pairs={{0,1},{1,2},{2,3},{3,4},{4,5},{5,6},{6,7},{8,9},{9,10},{10,11},{11... | collective-permute-start | bytes 491528 | tf_op jit(solution)/shard_map/ppermute | solution.py:15
  108.9 18.4 %collective-permute-start.1 = (bf16[2,1,64,640]{3,2,1,0:T(8,128)(2,1)S(1)}, bf16[2,1,64,640]{3,2,1,0:T(8,128)(2,1)S(1)}, u32[]{:S(2)}, u32[]{:S(2)}) collective-permute-start(bf16[2,1,64,640]{3,2,1,0:T(8,128)(2,1)S(1)} %copy-done), channel_id=1, source_target_pairs={{1,0},{2,1},{3,2},{4,3},{5,4},{6,5},{7,6},{9,8},{10,9},{11,10},{12... | collective-permute-start | bytes 491528 | tf_op jit(solution)/shard_map/ppermute | solution.py:18
  145.9 1.8 copy-start.4
  145.9 1.8 copy-start.6
  145.9 1.8 copy-start.7
  165.5 8.4 %collective-permute-start.2 = (bf16[2,1,64,640]{3,2,0,1:T(8,128)(2,1)S(1)}, bf16[2,1,64,640]{3,2,0,1:T(8,128)(2,1)S(1)}, u32[]{:S(2)}, u32[]{:S(2)}) collective-permute-start(bf16[2,1,64,640]{3,2,0,1:T(8,128)(2,1)S(1)} %fusion.50), channel_id=1, source_target_pairs={{0,1},{1,2},{2,3},{3,4},{4,5},{5,6},{6,7},{8,9},{9,10},{10,11},{11... | collective-permute-start | bytes 491528 | tf_op jit(solution)/shard_map/ppermute | solution.py:15
  167.5 7.4 %collective-permute-start.3 = (bf16[2,1,64,640]{3,2,0,1:T(8,128)(2,1)S(1)}, bf16[2,1,64,640]{3,2,0,1:T(8,128)(2,1)S(1)}, u32[]{:S(2)}, u32[]{:S(2)}) collective-permute-start(bf16[2,1,64,640]{3,2,0,1:T(8,128)(2,1)S(1)} %fusion.50), channel_id=1, source_target_pairs={{1,0},{2,1},{3,2},{4,3},{5,4},{6,5},{7,6},{9,8},{10,9},{11,10},{12... | collective-permute-start | bytes 491528 | tf_op jit(solution)/shard_map/ppermute | solution.py:18
  193.4 1.8 copy-start.2
  193.4 1.8 copy-start.8
  193.4 1.8 copy-start.9
Sparse Core Ops, SparseCore 0:
  57.9 50.5 all-gather.2
  110.4 50.1 all-gather.4
where the time goes:
time: 225 us; the launch traced here: 223 us
  blocking collectives  132 us (59%)
  local copies, waits for them, and re-layouts  50.2 us (22%)
  between operations  13.8 us (6%)
  starting transfers between devices  13.3 us (6%)
  matrix products  10 us (4%)
    all_gather x2, blocking collectives, conv_backward(): gathered = lax.all_gather(weights, 'dp', axis=1, tiled=True)  92.9 us
    another operation x20, local copies, waits for them, and re-layouts, conv_backward(): stacked = jnp.stack(shifted, axis=1)  36.9 us
    psum x2, blocking collectives, norm_backward(): lax.psum((group_sums(scaled), group_sums(scaled * normed)), 'rows')  26.5 us
    psum x1, blocking collectives, reduced_stats(): lax.psum((group_sums(values), group_sums(values * values)), 'rows')  12.3 us
    dot_general x2, matrix products, conv_backward(): result = jnp.dot(window, flat, preferred_element_type=jnp.float32)  10 us
    ppermute x2, starting transfers between devices, extended(): lax.ppermute(lax.slice_in_dim(block, 0, width, axis=dim), axis, backward)  9.26 us
    all_gather x2, local copies, waits for them, and re-layouts, conv_backward(): gathered = lax.all_gather(weights, 'dp', axis=1, tiled=True)  5.97 us
  transfers between devices with their start and end apart: 6, of which 2 were waited for; matrix products, arithmetic and copies ran while one was open for 23% of the time, Pallas kernels for 0%

commit v1 on v0

--- a/solution.py
+++ b/solution.py
@@ -68,7 +68,7 @@
         ]
         shifted.append(window.reshape(pixels, channels))
     stacked = jnp.stack(shifted, axis=1)
-    gathered = lax.all_gather(weights, "dp", axis=1, tiled=True)
+    gathered = jnp.concatenate(lax.all_gather(weights, "dp"), axis=1)
     section = lax.all_gather(gathered, "rows", axis=2, tiled=True)
     columns = section.shape[2]
     window = stacked.reshape(pixels, 9 * columns)

time: 225 us -> 195 us (0.87)
  blocking collectives: 132 us -> 99.8 us
  waiting for transfers between devices: 2.08 us -> 5.66 us
    all_gather x2, blocking collectives: 92.9 us -> 56.6 us  [conv_backward(): gathered = jnp.concatenate(lax.all_gather(weights, 'dp'), axis=1)]
    all_gather x2 -> x0, local copies, waits for them, and re-layouts: 5.97 us -> none  [conv_backward(): gathered = lax.all_gather(weights, 'dp', axis=1, tiled=True)]
    reshape x0 -> x4, local copies, waits for them, and re-layouts: none -> 5.67 us  [conv_backward(): gathered = jnp.concatenate(lax.all_gather(weights, 'dp'), axis=1)]
    ppermute x2, waiting for transfers between devices: 1.18 us -> 5.62 us  [extended(): lax.ppermute(lax.slice_in_dim(block, block.shape[dim] - width, None, axis...]
    psum x1, blocking collectives: 12.3 us -> 16.5 us  [reduced_stats(): lax.psum((group_sums(values), group_sums(values * values)), 'rows')]
  transfers between devices with their start and end apart: 6 -> 6, of which waited for: 2 -> 1; matrix products, arithmetic and copies ran while one was open for 23% -> 27% of each run, Pallas kernels for 0% -> 0%
where the time goes in v1:
time: 195 us; the launch traced here: 193 us
  blocking collectives  99.8 us (51%)
  local copies, waits for them, and re-layouts  48.5 us (25%)
  between operations  13.8 us (7%)
  starting transfers between devices  13.3 us (7%)
  matrix products  9.89 us (5%)
  waiting for transfers between devices  5.66 us (3%)
  other arithmetic  2.04 us (1%)
    all_gather x2, blocking collectives, conv_backward(): gathered = jnp.concatenate(lax.all_gather(weights, 'dp'), axis=1)  56.6 us
    another operation x20, local copies, waits for them, and re-layouts, conv_backward(): stacked = jnp.stack(shifted, axis=1)  36.9 us
    psum x2, blocking collectives, norm_backward(): lax.psum((group_sums(scaled), group_sums(scaled * normed)), 'rows')  26.6 us
    psum x1, blocking collectives, reduced_stats(): lax.psum((group_sums(values), group_sums(values * values)), 'rows')  16.5 us
    dot_general x2, matrix products, conv_backward(): result = jnp.dot(window, flat, preferred_element_type=jnp.float32)  9.89 us
    ppermute x2, starting transfers between devices, extended(): lax.ppermute(lax.slice_in_dim(block, 0, width, axis=dim), axis, backward)  9.26 us
    reshape x4, local copies, waits for them, and re-layouts, conv_backward(): gathered = jnp.concatenate(lax.all_gather(weights, 'dp'), axis=1)  5.67 us
    ppermute x2, waiting for transfers between devices, extended(): lax.ppermute(lax.slice_in_dim(block, block.shape[dim] - width, None, axis...  5.62 us
  transfers between devices with their start and end apart: 6, of which 1 were waited for; matrix products, arithmetic and copies ran while one was open for 27% of the time, Pallas kernels for 0%

profile of v1, /device:TPU:28, one launch (start us, length us, event | category | flops | bytes accessed | tf_op | source)
XLA Modules:
  0.0 192.9 jit_solution(15293250995902167997)
XLA Ops:
  6.5 28.8 %all-gather = bf16[36,160,80]{2,1,0:T(8,128)(2,1)S(1)} all-gather(bf16[9,160,80]{2,1,0:T(8,128)(2,1)} %param.13), channel_id=2, replica_groups=mesh['dp'=4,'rows'=8] {'dp'}, dimensions={0}, use_global_device_ids=true | all-gather | bytes 1152000 | tf_op jit(solution)/shard_map/all_gather | solution.py:71
  35.3 1.1 copy.86
  36.5 1.7 reshape.102
  38.2 27.9 %all-gather.1 = bf16[36,160,80]{2,1,0:T(8,128)(2,1)S(1)} all-gather(bf16[9,160,80]{2,1,0:T(8,128)(2,1)S(1)} %copy-done.5), channel_id=3, replica_groups=mesh['dp'=4,'rows'=8] {'dp'}, dimensions={0}, use_global_device_ids=true | all-gather | bytes 1152000 | tf_op jit(solution)/shard_map/all_gather | solution.py:71
  66.1 1.1 copy.96
  67.3 1.7 reshape.108
  69.0 2.1 %collective-permute-start = (bf16[2,1,64,640]{3,2,1,0:T(8,128)(2,1)S(1)}, bf16[2,1,64,640]{3,2,1,0:T(8,128)(2,1)S(1)}, u32[]{:S(2)}, u32[]{:S(2)}) collective-permute-start(bf16[2,1,64,640]{3,2,1,0:T(8,128)(2,1)S(1)} %copy-done), channel_id=1, source_target_pairs={{0,1},{1,2},{2,3},{3,4},{4,5},{5,6},{6,7},{8,9},{9,10},{10,11},{11... | collective-permute-start | bytes 491528 | tf_op jit(solution)/shard_map/ppermute | solution.py:15
  71.1 4.5 %collective-permute-start.1 = (bf16[2,1,64,640]{3,2,1,0:T(8,128)(2,1)S(1)}, bf16[2,1,64,640]{3,2,1,0:T(8,128)(2,1)S(1)}, u32[]{:S(2)}, u32[]{:S(2)}) collective-permute-start(bf16[2,1,64,640]{3,2,1,0:T(8,128)(2,1)S(1)} %copy-done), channel_id=1, source_target_pairs={{1,0},{2,1},{3,2},{4,3},{5,4},{6,5},{7,6},{9,8},{10,9},{11,10},{12... | collective-permute-start | bytes 491528 | tf_op jit(solution)/shard_map/ppermute | solution.py:18
  75.8 0.1 reshape.99
  75.9 0.1 reduce_sum.149
  76.0 0.1 reduce_sum.151
  76.1 16.5 %all-reduce.4 = (f32[2,16]{1,0:T(2,128)S(1)}, f32[2,16]{1,0:T(2,128)S(1)}) all-reduce(f32[2,16]{1,0:T(2,128)S(1)} %reduce_sum.151, f32[2,16]{1,0:T(2,128)S(1)} %reduce_sum.149), channel_id=1, replica_groups=mesh['dp'=4,'rows'=8] {'rows'}, use_global_device_ids=true, to_apply=%region_11.12 | all-reduce | flops 64 | bytes 512 | tf_op jit(solution)/shard_map/psum | solution.py:40
  92.6 0.3 copy.81
  92.9 0.1 mul.122
  93.1 0.1 sub.60
  93.4 0.1 reduce_sum.145
  93.4 0.1 reshape.97
  93.5 0.1 reduce_sum.147
  93.6 0.2 fusion.15
  93.8 0.2 fusion.55
  94.0 0.3 copy.77
  94.2 1.0 copy.79
  95.2 1.0 copy.80
  96.2 1.0 copy.82
  97.1 1.0 copy.83
  98.1 1.0 copy.85
  99.1 1.0 copy.78
  100.1 1.0 copy.84
  101.1 11.1 %stack.6 = bf16[128,9,640]{2,1,0:T(8,128)(2,1)S(1)} concatenate(bf16[128,1,640]{2,1,0:T(2,128)(2,1)S(1)} %copy.77, bf16[128,1,640]{2,1,0:T(2,128)(2,1)} %copy.78, bf16[128,1,640]{2,1,0:T(2,128)(2,1)} %copy.79, bf16[128,1,640]{2,1,0:T(2,128)(2,1)} %copy.80, bf16[128,1,640]{2,1,0:T(2,128)(2,1)S(1)} %copy.81, bf16[128,1,640]{2,1,0:T(2,128)(2,1)} %copy.82, ...), dimensions={1} | concatenate | bytes 2949120 | tf_op jit(solution)/shard_map/stack | solution.py:70
  112.2 1.8 reshape.100
  114.0 5.0 %fusion.53 = (f32[2,640]{1,0:T(2,128)S(1)}, f32[2,640]{1,0:T(2,128)S(1)}, f32[2,1,64,640]{3,2,0,1:T(8,128)S(1)}) fusion(f32[2,640]{1,0:T(2,128)S(1)} %mul.122, f32[2,640]{1,0:T(2,128)S(1)} %sub.60, bf16[2,1,64,640]{3,2,1,0:T(8,128)(2,1)S(1)} %copy-done.4, f32[640]{0:T(1024)S(1)} %copy-done.6, f32[640]{0:T(1024)S(1)} %copy-done.7, ...), kind=kOutput, calls=%fused_computation.73 | convolution fusion | flops 945108480 | bytes 9364480 | tf_op jit(solution)/shard_map/dot_general | solution.py:76
  119.0 0.1 reduce_sum.153
  119.1 0.1 reshape.105
  119.2 0.1 reduce_sum.155
  119.3 12.6 %all-reduce.3 = (f32[2,16]{1,0:T(2,128)S(1)}, f32[2,16]{1,0:T(2,128)S(1)}, f32[2,16]{1,0:T(2,128)S(1)}, f32[2,16]{1,0:T(2,128)S(1)}) all-reduce(f32[2,16]{1,0:T(2,128)S(1)} %reduce_sum.155, f32[2,16]{1,0:T(2,128)S(1)} %reduce_sum.153, f32[2,16]{1,0:T(2,128)S(1)} %reduce_sum.147, ...), channel_id=1, replica_groups=mesh['dp'=4,'rows'=8] {'rows'}, use_global_device_ids=true, to_apply=%region_17.18 | all-reduce | flops 128 | bytes 1024 | tf_op jit(solution)/shard_map/psum | solution.py:51
  132.0 0.1 mul.132
  132.2 0.1 sub.64
  132.3 0.1 fusion.50
  132.4 1.9 collective-permute-start.2
  134.3 4.7 %collective-permute-start.3 = (bf16[2,1,64,640]{3,2,0,1:T(8,128)(2,1)S(1)}, bf16[2,1,64,640]{3,2,0,1:T(8,128)(2,1)S(1)}, u32[]{:S(2)}, u32[]{:S(2)}) collective-permute-start(bf16[2,1,64,640]{3,2,0,1:T(8,128)(2,1)S(1)} %fusion.50), channel_id=1, source_target_pairs={{1,0},{2,1},{3,2},{4,3},{5,4},{6,5},{7,6},{9,8},{10,9},{11,10},{12... | collective-permute-start | bytes 491528 | tf_op jit(solution)/shard_map/ppermute | solution.py:18
  139.0 0.3 copy.91
  139.3 0.1 mul.118
  139.5 0.1 sub.68
  139.6 5.6 %collective-permute-done.2 = bf16[2,1,64,640]{3,2,0,1:T(8,128)(2,1)S(1)} collective-permute-done((bf16[2,1,64,640]{3,2,0,1:T(8,128)(2,1)S(1)}, bf16[2,1,64,640]{3,2,0,1:T(8,128)(2,1)S(1)}, u32[]{:S(2)}, u32[]{:S(2)}) %collective-permute-start.2) | collective-permute-done | bytes 163872 | tf_op jit(solution)/shard_map/ppermute | solution.py:15
  145.2 0.2 fusion.17
  145.4 0.2 fusion.54
  145.5 0.3 copy.87
  145.8 1.0 copy.89
  146.8 1.0 copy.90
  147.8 1.0 copy.92
  148.8 1.0 copy.93
  149.8 1.0 copy.95
  150.7 1.0 copy.88
  151.7 1.0 copy.94
  152.7 11.0 %stack.7 = bf16[128,9,640]{2,1,0:T(8,128)(2,1)S(1)} concatenate(bf16[128,1,640]{2,1,0:T(2,128)(2,1)S(1)} %copy.87, bf16[128,1,640]{2,1,0:T(2,128)(2,1)} %copy.88, bf16[128,1,640]{2,1,0:T(2,128)(2,1)} %copy.89, bf16[128,1,640]{2,1,0:T(2,128)(2,1)} %copy.90, bf16[128,1,640]{2,1,0:T(2,128)(2,1)S(1)} %copy.91, bf16[128,1,640]{2,1,0:T(2,128)(2,1)} %copy.92, ...), dimensions={1} | concatenate | bytes 2949120 | tf_op jit(solution)/shard_map/stack | solution.py:70
  163.8 1.8 reshape.106
  165.6 4.9 %fusion.52 = (f32[2,640]{1,0:T(2,128)S(1)}, f32[2,640]{1,0:T(2,128)S(1)}, f32[2,1,64,640]{3,2,0,1:T(8,128)S(1)}) fusion(f32[2,640]{1,0:T(2,128)S(1)} %mul.118, f32[2,640]{1,0:T(2,128)S(1)} %sub.68, bf16[2,1,64,640]{3,2,1,0:T(8,128)(2,1)S(1)} %copy-done.2, f32[640]{0:T(1024)S(1)} %copy-done.8, f32[640]{0:T(1024)S(1)} %copy-done.9, ...), kind=kOutput, calls=%fused_computation.72 | convolution fusion | flops 945108480 | bytes 9364480 | tf_op jit(solution)/shard_map/dot_general | solution.py:76
  170.7 0.1 reduce_sum.157
  170.7 0.1 reshape.111
  170.8 0.1 reduce_sum.159
  170.9 14.0 %all-reduce.2 = (f32[2,16]{1,0:T(2,128)S(1)}, f32[2,16]{1,0:T(2,128)S(1)}) all-reduce(f32[2,16]{1,0:T(2,128)S(1)} %reduce_sum.159, f32[2,16]{1,0:T(2,128)S(1)} %reduce_sum.157), channel_id=1, replica_groups=mesh['dp'=4,'rows'=8] {'rows'}, use_global_device_ids=true, to_apply=%region_23.24 | all-reduce | flops 64 | bytes 512 | tf_op jit(solution)/shard_map/psum | solution.py:51
  185.0 0.1 mul.144
  185.2 0.1 sub.72
  185.3 0.8 fusion.51
  (48 shorter events, 1.2 us)
Async XLA Ops:
  6.5 107.4 %all-gather.5.cloned.1.call-start = ((), (), s32[]{:S(2)}) async-start(), calls=%async_computation | async-start | bytes 8294400 | tf_op jit(solution)/shard_map/all_gather | solution.py:72
  36.4 1.8 copy-start.5
  38.2 127.4 %all-gather.7.cloned.1.call-start = ((), (), s32[]{:S(2)}) async-start(), calls=%async_computation.1 | async-start | bytes 8294400 | tf_op jit(solution)/shard_map/all_gather | solution.py:72
  67.3 1.8 copy-start
  67.3 8.4 %copy-start.3 = (bf16[2,1,64,640]{3,2,1,0:T(8,128)(2,1)S(1)}, bf16[2,1,64,640]{3,2,1,0:T(8,128)(2,1)}, u32[]{:S(2)}) copy-start(bf16[2,1,64,640]{3,2,1,0:T(8,128)(2,1)} %param.10) | copy-start | bytes 491524
  69.0 24.2 %copy-start.1 = (bf16[2,1,64,640]{3,2,1,0:T(8,128)(2,1)S(1)}, bf16[2,1,64,640]{3,2,1,0:T(8,128)(2,1)}, u32[]{:S(2)}) copy-start(bf16[2,1,64,640]{3,2,1,0:T(8,128)(2,1)} %param.9) | copy-start | bytes 491524
  69.0 24.6 %collective-permute-start = (bf16[2,1,64,640]{3,2,1,0:T(8,128)(2,1)S(1)}, bf16[2,1,64,640]{3,2,1,0:T(8,128)(2,1)S(1)}, u32[]{:S(2)}, u32[]{:S(2)}) collective-permute-start(bf16[2,1,64,640]{3,2,1,0:T(8,128)(2,1)S(1)} %copy-done), channel_id=1, source_target_pairs={{0,1},{1,2},{2,3},{3,4},{4,5},{5,6},{6,7},{8,9},{9,10},{10,11},{11... | collective-permute-start | bytes 491528 | tf_op jit(solution)/shard_map/ppermute | solution.py:15
  71.1 22.5 %collective-permute-start.1 = (bf16[2,1,64,640]{3,2,1,0:T(8,128)(2,1)S(1)}, bf16[2,1,64,640]{3,2,1,0:T(8,128)(2,1)S(1)}, u32[]{:S(2)}, u32[]{:S(2)}) collective-permute-start(bf16[2,1,64,640]{3,2,1,0:T(8,128)(2,1)S(1)} %copy-done), channel_id=1, source_target_pairs={{1,0},{2,1},{3,2},{4,3},{5,4},{6,5},{7,6},{9,8},{10,9},{11,10},{12... | collective-permute-start | bytes 491528 | tf_op jit(solution)/shard_map/ppermute | solution.py:18
  112.2 1.8 copy-start.4
  112.2 1.8 copy-start.6
  112.2 1.8 copy-start.7
  132.4 12.9 %collective-permute-start.2 = (bf16[2,1,64,640]{3,2,0,1:T(8,128)(2,1)S(1)}, bf16[2,1,64,640]{3,2,0,1:T(8,128)(2,1)S(1)}, u32[]{:S(2)}, u32[]{:S(2)}) collective-permute-start(bf16[2,1,64,640]{3,2,0,1:T(8,128)(2,1)S(1)} %fusion.50), channel_id=1, source_target_pairs={{0,1},{1,2},{2,3},{3,4},{4,5},{5,6},{6,7},{8,9},{9,10},{10,11},{11... | collective-permute-start | bytes 491528 | tf_op jit(solution)/shard_map/ppermute | solution.py:15
  134.3 10.9 %collective-permute-start.3 = (bf16[2,1,64,640]{3,2,0,1:T(8,128)(2,1)S(1)}, bf16[2,1,64,640]{3,2,0,1:T(8,128)(2,1)S(1)}, u32[]{:S(2)}, u32[]{:S(2)}) collective-permute-start(bf16[2,1,64,640]{3,2,0,1:T(8,128)(2,1)S(1)} %fusion.50), channel_id=1, source_target_pairs={{1,0},{2,1},{3,2},{4,3},{5,4},{6,5},{7,6},{9,8},{10,9},{11,10},{12... | collective-permute-start | bytes 491528 | tf_op jit(solution)/shard_map/ppermute | solution.py:18
  163.8 1.8 copy-start.2
  163.8 1.8 copy-start.8
  163.8 1.8 copy-start.9
Sparse Core Ops, SparseCore 0:
  38.3 52.6 all-gather.4
  92.9 53.3 all-gather.6
